TPU v7x, 32 devices: a whole 2x2x4 slice. The times are simulated.
32 devices in a mesh: dp: 4 (over y, x), tensor: 8 (over z, core).
Axes of the slice: x: 2, y: 2, z: 4, core: 2. Of those that a mesh axis runs over, the one named last changes fastest.
Arguments:
- tokens: bfloat16 [2048, 2048], P(('dp', 'tensor')), may hold values from -12 to 12
- targets: bfloat16 [2048, 2048], P(('dp', 'tensor')), may hold values from -6 to 6
- learner_gain: float32 [2048], replicated, may hold values from 0.1 to 1.9
- learner_gate: bfloat16 [2048, 8192], P(None, 'tensor'), may hold values from -0.125 to 0.125
- learner_up: bfloat16 [2048, 8192], P(None, 'tensor'), may hold values from -0.125 to 0.125
- learner_down: bfloat16 [8192, 2048], P('tensor'), may hold values from -0.0625 to 0.0625
- frozen_gain: float32 [2048], replicated, may hold values from 0.1 to 1.9
- frozen_gate: bfloat16 [2048, 8192], P(None, 'tensor'), may hold values from -0.125 to 0.125
- frozen_up: bfloat16 [2048, 8192], P(None, 'tensor'), may hold values from -0.125 to 0.125
- frozen_down: bfloat16 [8192, 2048], P('tensor'), may hold values from -0.0625 to 0.0625
Outputs:
- scores: float32 [2048], P(('dp', 'tensor'))
- grad_tokens: bfloat16 [2048, 2048], P(('dp', 'tensor'))
- grad_gain: float32 [2048], replicated
- grad_gate: float32 [2048, 8192], P('dp', 'tensor')
- grad_up: float32 [2048, 8192], P('dp', 'tensor')
- grad_down: float32 [8192, 2048], P('tensor', 'dp')
All inputs are finite; a program needn't handle non-finite values.
Results may differ from a plain program's by a relative error of at most 0.0096.
Values may be sent and summed in bfloat16 or wider, within the bound.
No kernel may reach another device: no remote copies, remote signals or barrier semaphores. Data moves between devices by JAX's collectives and lax.ppermute only.
A program may use at most 128 MiB of HBM per device.

v0:
```python
import math

import jax
import jax.numpy as jnp
from jax import lax
from jax.sharding import PartitionSpec as P


def project_up(normed, w_gate, w_up, w_down):
    gate_pre = jnp.dot(normed, w_gate, preferred_element_type=jnp.float32)
    up_pre = jnp.dot(normed, w_up, preferred_element_type=jnp.float32)
    hidden = (jax.nn.silu(gate_pre) * up_pre).astype(jnp.bfloat16)
    partial_out = jnp.dot(hidden, w_down, preferred_element_type=jnp.float32)
    return (gate_pre, up_pre, hidden, partial_out)


def local(
    tokens,
    targets,
    learner_gain,
    learner_gate,
    learner_up,
    learner_down,
    frozen_gain,
    frozen_gate,
    frozen_up,
    frozen_down,
):
    xfloat = tokens.astype(jnp.float32)
    inv_rms = lax.rsqrt(jnp.mean(xfloat * xfloat, axis=-1, keepdims=True) + 1e-05)
    normed = (xfloat * inv_rms * learner_gain).astype(jnp.bfloat16)
    frozen_normed = (xfloat * inv_rms * frozen_gain).astype(jnp.bfloat16)
    normed_all, frozen_all = (
        lax.all_gather(normed, "tensor", axis=0, tiled=True),
        lax.all_gather(frozen_normed, "tensor", axis=0, tiled=True),
    )
    gate_pre, up_pre, hidden, partial_learned = project_up(
        normed_all, learner_gate, learner_up, learner_down
    )
    frozen_partial = project_up(frozen_all, frozen_gate, frozen_up, frozen_down)[3]
    learned, frozen_out = (
        lax.psum_scatter(partial_learned, "tensor", scatter_dimension=0, tiled=True),
        lax.psum_scatter(frozen_partial, "tensor", scatter_dimension=0, tiled=True),
    )
    goal = targets.astype(jnp.float32)
    root = math.sqrt(tokens.shape[1])
    miss = learned - goal
    frozen_miss = frozen_out - goal
    learner_loss = 0.5 * jnp.sum(miss * miss, axis=-1) / root
    frozen_loss = 0.5 * jnp.sum(frozen_miss * frozen_miss, axis=-1) / root
    scores = learner_loss - frozen_loss
    weight = jax.nn.sigmoid(scores)
    out_grad = (weight[:, None] * miss / root).astype(jnp.bfloat16)
    grads_all = lax.all_gather(out_grad, "tensor", axis=0, tiled=True)
    hidden_grad = jnp.dot(grads_all, learner_down.T, preferred_element_type=jnp.float32)
    sigma = jax.nn.sigmoid(gate_pre)
    gate_grad = (hidden_grad * up_pre * sigma * (1.0 + gate_pre * (1.0 - sigma))).astype(
        jnp.bfloat16
    )
    up_grad = (hidden_grad * gate_pre * sigma).astype(jnp.bfloat16)
    partial_normed = jnp.dot(
        gate_grad, learner_gate.T, preferred_element_type=jnp.float32
    ) + jnp.dot(up_grad, learner_up.T, preferred_element_type=jnp.float32)
    normed_grad = lax.psum_scatter(partial_normed, "tensor", scatter_dimension=0, tiled=True)
    gain_term = jnp.sum(normed_grad * xfloat * inv_rms, axis=0)
    grad_gain = lax.psum(gain_term, ("dp", "tensor"))
    scaled = learner_gain * normed_grad
    cubed = inv_rms * inv_rms * inv_rms
    grad_tokens = (
        inv_rms * scaled - xfloat * cubed * jnp.mean(scaled * xfloat, axis=-1, keepdims=True)
    ).astype(jnp.bfloat16)
    normed_cols, grad_cols = (
        lax.all_to_all(normed_all, "dp", split_axis=1, concat_axis=0, tiled=True),
        lax.all_to_all(grads_all, "dp", split_axis=1, concat_axis=0, tiled=True),
    )
    gate_piece = lax.all_gather(gate_grad, "dp", axis=0, tiled=True)
    up_piece = lax.all_gather(up_grad, "dp", axis=0, tiled=True)
    hidden_piece = lax.all_gather(hidden, "dp", axis=0, tiled=True)
    grad_gate = jnp.einsum("td,tf->df", normed_cols, gate_piece, preferred_element_type=jnp.float32)
    grad_up = jnp.einsum("td,tf->df", normed_cols, up_piece, preferred_element_type=jnp.float32)
    grad_down = jnp.einsum("tf,td->fd", hidden_piece, grad_cols, preferred_element_type=jnp.float32)
    return (scores, grad_tokens, grad_gain, grad_gate, grad_up, grad_down)


def solution(mesh):
    placed = (
        P(("dp", "tensor"), None),
        P(("dp", "tensor"), None),
        P(),
        P(None, "tensor"),
        P(None, "tensor"),
        P("tensor", None),
        P(),
        P(None, "tensor"),
        P(None, "tensor"),
        P("tensor", None),
    )
    return jax.shard_map(
        local,
        mesh=mesh,
        in_specs=placed,
        out_specs=(
            P(("dp", "tensor")),
            P(("dp", "tensor"), None),
            P(),
            P("dp", "tensor"),
            P("dp", "tensor"),
            P("tensor", "dp"),
        ),
        check_vma=False,
    )
```

profile of v0, /device:TPU:12, one launch (start us, length us, event | category | flops | bytes accessed | tf_op | source)
XLA Modules:
  0.0 501.6 jit_solution(8420820339097003614)
XLA Ops:
  7.2 0.0 all-gather.7.cloned.1.call-start
  7.2 1.1 fusion.7
  8.3 1.9 fusion.4
  10.3 0.0 all-gather.9.cloned.1.call-start
  10.3 0.7 all-gather.9.cloned.1.call-update
  11.0 0.0 reduce-scatter.4.cloned.1.call-start
  11.1 29.6 %all-gather.7.cloned.1.call-done = bf16[512,2048]{1,0:T(8,128)(2,1)} async-done(((bf16[64,2048]{1,0:T(8,128)(2,1)}), bf16[512,2048]{1,0:T(8,128)(2,1)}) %all-gather.7.cloned.1.call-update) | async-done | bytes 2097168 | tf_op jit(solution)/shard_map/all_gather | solution.py:34
  40.7 5.3 %fusion.15 = f32[512,1024]{1,0:T(8,128)S(1)} fusion(bf16[512,2048]{1,0:T(8,128)(2,1)} %all-gather.7.cloned.1.call-done, bf16[2048,1024]{1,0:T(8,128)(2,1)} %param.13), kind=kOutput, calls=%fused_computation.37 | convolution fusion | flops 2147483648 | bytes 8388608 | tf_op jit(solution)/shard_map/dot_general | solution.py:10
  46.0 3.8 multiply_convert_fusion.3
  49.8 6.9 %fusion.16 = f32[512,2048]{1,0:T(8,128)} fusion(bf16[512,1024]{1,0:T(8,128)(2,1)S(1)} %get-tuple-element.18, bf16[1024,2048]{1,0:T(8,128)(2,1)} %param.15), kind=kOutput, calls=%fused_computation.38 | convolution fusion | flops 2147483648 | bytes 9437184 | tf_op jit(solution)/shard_map/dot_general | solution.py:13
  56.7 0.0 reduce-scatter.4.cloned.1.call-update
  56.7 0.0 reduce-scatter.6.cloned.1.call-start
  56.8 14.7 %all-gather.9.cloned.1.call-done = bf16[512,2048]{1,0:T(8,128)(2,1)} async-done(((bf16[64,2048]{1,0:T(8,128)(2,1)}), bf16[512,2048]{1,0:T(8,128)(2,1)}) %all-gather.9.cloned.1.call-update) | async-done | bytes 2097168 | tf_op jit(solution)/shard_map/all_gather | solution.py:35
  71.4 6.6 %fusion.17 = f32[512,1024]{1,0:T(8,128)} fusion(bf16[512,2048]{1,0:T(8,128)(2,1)} %all-gather.9.cloned.1.call-done, bf16[2048,1024]{1,0:T(8,128)(2,1)} %param.17), kind=kOutput, calls=%fused_computation.39 | convolution fusion | flops 2147483648 | bytes 8388608 | tf_op jit(solution)/shard_map/dot_general | solution.py:10
  78.1 11.0 %fusion = f32[512,2048]{1,0:T(8,128)} fusion(bf16[1024,2048]{1,0:T(8,128)(2,1)} %param.19, f32[512,1024]{1,0:T(8,128)} %fusion.17, bf16[512,2048]{1,0:T(8,128)(2,1)S(1)} %copy-done.10, bf16[2048,1024]{1,0:T(8,128)(2,1)} %param.18), kind=kOutput, calls=%fused_computation.13 | convolution fusion | flops 4298113024 | bytes 16777216 | tf_op jit(solution)/shard_map/dot_general | solution.py:13
  89.1 0.0 all-gather.11.cloned.1.call-start
  89.1 30.8 %reduce-scatter.4.cloned.1.call-done = f32[64,2048]{1,0:T(8,128)} async-done(((f32[512,2048]{1,0:T(8,128)}), f32[64,2048]{1,0:T(8,128)}) %reduce-scatter.4.cloned.1.call-update) | async-done | bytes 524304 | tf_op jit(solution)/shard_map/reduce_scatter | solution.py:42
  120.0 50.6 %reduce-scatter.6.cloned.1.call-done = f32[64,2048]{1,0:T(8,128)} async-done(((f32[512,2048]{1,0:T(8,128)}), f32[64,2048]{1,0:T(8,128)}) %reduce-scatter.6.cloned.1.call-update) | async-done | bytes 524304 | tf_op jit(solution)/shard_map/reduce_scatter | solution.py:43
  170.6 1.4 multiply_reduce_fusion
  172.0 0.5 add_divide_fusion.1
  172.5 1.9 multiply_convert_fusion.4
  174.4 0.0 all-gather.17.cloned.1.call-start
  174.4 0.5 all-gather.17.cloned.1.call-update
  175.0 0.2 all-gather.13.cloned.1.call-start
  175.2 30.1 %all-gather.11.cloned.1.call-done = bf16[512,2048]{1,0:T(8,128)(2,1)} async-done(((bf16[64,2048]{1,0:T(8,128)(2,1)}), bf16[512,2048]{1,0:T(8,128)(2,1)}) %all-gather.11.cloned.1.call-update) | async-done | bytes 2097168 | tf_op jit(solution)/shard_map/all_gather | solution.py:54
  205.3 8.3 %multiply_convert_fusion = (bf16[512,1024]{1,0:T(8,128)(2,1)}, bf16[512,1024]{1,0:T(8,128)(2,1)}) fusion(f32[512,1024]{1,0:T(8,128)} %copy-done.11, f32[512,1024]{1,0:T(8,128)} %get-tuple-element.19, bf16[512,2048]{1,0:T(8,128)(2,1)} %all-gather.11.cloned.1.call-done, bf16[1024,2048]{1,0:T(8,128)(2,1)} %param.15), kind=kOutput, calls=%fused_computation.3 | convolution fusion | flops 2154299392 | bytes 12582912 | tf_op jit(solution)/shard_map/dot_general | solution.py:55
  213.6 0.0 all-gather.15.cloned.1.call-start
  213.6 0.7 all-gather.15.cloned.1.call-update
  214.4 0.0 reduce-scatter.8.cloned.1.call-start
  214.4 0.5 copy-done.5
  214.9 5.0 fusion.18
  220.0 4.3 convolution_add_fusion
  224.3 1.6 copy-done.2
  225.9 1.5 copy.22
  227.4 4.2 all-to-all-start.1
  231.6 3.1 copy.23
  234.7 42.9 %all-to-all-done.1 = bf16[512,4,512]{2,0,1:T(8,128)(2,1)S(1)} async-done(((bf16[512,4,512]{2,0,1:T(8,128)(2,1)}), bf16[512,4,512]{2,0,1:T(8,128)(2,1)S(1)}, u32[]{:S(2)}, u32[]{:S(2)}) %all-to-all-start.1) | async-done | bytes 2097184 | tf_op jit(solution)/shard_map/all_to_all | solution.py:74
  277.6 5.0 all-to-all-start
  282.6 5.9 %fusion.21 = f32[1024,512]{1,0:T(8,128)} fusion(bf16[2048,1024]{1,0:T(8,128)(2,1)} %all-gather.17.cloned.1.call-done, bf16[2048,512]{1,0:T(8,128)(2,1)S(1)} %bitcast.37), kind=kOutput, calls=%fused_computation.43 | convolution fusion | flops 2147483648 | bytes 8388608 | tf_op jit(solution)/shard_map/tf,td->fd/dot_general | solution.py:81
  288.5 28.0 %all-to-all-done = bf16[512,4,512]{2,0,1:T(8,128)(2,1)} async-done(((bf16[512,4,512]{2,0,1:T(8,128)(2,1)}), bf16[512,4,512]{2,0,1:T(8,128)(2,1)}, u32[]{:S(2)}, u32[]{:S(2)}) %all-to-all-start) | async-done | bytes 2097184 | tf_op jit(solution)/shard_map/all_to_all | solution.py:73
  316.4 28.3 %all-gather.13.cloned.1.call-done = bf16[2048,1024]{1,0:T(8,128)(2,1)} async-done(((bf16[512,1024]{1,0:T(8,128)(2,1)}), bf16[2048,1024]{1,0:T(8,128)(2,1)}) %all-gather.13.cloned.1.call-update) | async-done | bytes 4194320 | tf_op jit(solution)/shard_map/all_gather | solution.py:76
  344.8 6.5 %fusion.19 = f32[512,1024]{1,0:T(8,128)} fusion(bf16[2048,512]{1,0:T(8,128)(2,1)} %bitcast.1, bf16[2048,1024]{1,0:T(8,128)(2,1)} %all-gather.13.cloned.1.call-done), kind=kOutput, calls=%fused_computation.41 | convolution fusion | flops 2147483648 | bytes 8388608 | tf_op jit(solution)/shard_map/td,tf->df/dot_general | solution.py:79
  351.3 48.0 %all-gather.15.cloned.1.call-done = bf16[2048,1024]{1,0:T(8,128)(2,1)} async-done(((bf16[512,1024]{1,0:T(8,128)(2,1)}), bf16[2048,1024]{1,0:T(8,128)(2,1)}) %all-gather.15.cloned.1.call-update) | async-done | bytes 4194320 | tf_op jit(solution)/shard_map/all_gather | solution.py:77
  399.2 6.5 %fusion.20 = f32[512,1024]{1,0:T(8,128)} fusion(bf16[2048,512]{1,0:T(8,128)(2,1)} %bitcast.1, bf16[2048,1024]{1,0:T(8,128)(2,1)} %all-gather.15.cloned.1.call-done), kind=kOutput, calls=%fused_computation.42 | convolution fusion | flops 2147483648 | bytes 8388608 | tf_op jit(solution)/shard_map/td,tf->df/dot_general | solution.py:80
  405.7 42.6 %reduce-scatter.8.cloned.1.call-done = f32[64,2048]{1,0:T(8,128)} async-done(((f32[512,2048]{1,0:T(8,128)}), f32[64,2048]{1,0:T(8,128)}) %reduce-scatter.8.cloned.1.call-update) | async-done | bytes 524304 | tf_op jit(solution)/shard_map/reduce_scatter | solution.py:64
  448.4 1.3 fusion.13
  449.7 43.4 %psum.7 = f32[2048]{0:T(1024)} all-reduce(f32[2048]{0:T(1024)S(1)} %get-tuple-element.6), channel_id=1, replica_groups=mesh['dp'=4,'tensor'=8] {'dp','tensor'}, use_global_device_ids=true, to_apply=%region_8.9 | all-reduce | flops 2048 | bytes 16384 | tf_op jit(solution)/shard_map/psum | solution.py:66
  493.1 1.9 fusion.10
  (30 shorter events, 0.1 us)
Async XLA Ops:
  7.2 33.5 %all-gather.7.cloned.1.call-start = ((), (), s32[]{:S(2)}) async-start(), calls=%async_computation.5 | async-start | bytes 2359296 | tf_op jit(solution)/shard_map/all_gather | solution.py:34
  10.3 61.2 %all-gather.9.cloned.1.call-start = ((), (), s32[]{:S(2)}) async-start(), calls=%async_computation.7 | async-start | bytes 2359296 | tf_op jit(solution)/shard_map/all_gather | solution.py:35
  11.0 108.9 %reduce-scatter.4.cloned.1.call-start = ((), (), s32[]{:S(2)}) async-start(), calls=%async_computation.6 | async-start | bytes 4718592 | tf_op jit(solution)/shard_map/reduce_scatter | solution.py:42
  40.7 5.3 %copy-start.1 = (bf16[512,2048]{1,0:T(8,128)(2,1)S(1)}, bf16[512,2048]{1,0:T(8,128)(2,1)}, u32[]{:S(2)}) copy-start(bf16[512,2048]{1,0:T(8,128)(2,1)} %all-gather.7.cloned.1.call-done) | copy-start | bytes 6291460
  40.7 5.3 %copy-start.8 = (bf16[2048,1024]{1,0:T(8,128)(2,1)S(1)}, bf16[2048,1024]{1,0:T(8,128)(2,1)}, u32[]{:S(2)}) copy-start(bf16[2048,1024]{1,0:T(8,128)(2,1)} %param.14) | copy-start | bytes 12582916
  46.0 3.8 copy-start.11
  49.8 6.9 %copy-start.3 = (bf16[512,1024]{1,0:T(8,128)(2,1)}, bf16[512,1024]{1,0:T(8,128)(2,1)S(1)}, u32[]{:S(2)}) copy-start(bf16[512,1024]{1,0:T(8,128)(2,1)S(1)} %get-tuple-element.18) | copy-start | bytes 3145732
  56.7 113.8 %reduce-scatter.6.cloned.1.call-start = ((), (), s32[]{:S(2)}) async-start(), calls=%async_computation.8 | async-start | bytes 4718592 | tf_op jit(solution)/shard_map/reduce_scatter | solution.py:43
  71.4 6.6 %copy-start.10 = (bf16[512,2048]{1,0:T(8,128)(2,1)S(1)}, bf16[512,2048]{1,0:T(8,128)(2,1)}, u32[]{:S(2)}) copy-start(bf16[512,2048]{1,0:T(8,128)(2,1)} %all-gather.9.cloned.1.call-done) | copy-start | bytes 6291460
  89.1 81.5 %copy-start.6 = (bf16[64,2048]{1,0:T(8,128)(2,1)S(1)}, bf16[64,2048]{1,0:T(8,128)(2,1)}, u32[]{:S(2)}) copy-start(bf16[64,2048]{1,0:T(8,128)(2,1)} %param.11) | copy-start | bytes 786436
  89.1 116.2 %all-gather.11.cloned.1.call-start = ((), (), s32[]{:S(2)}) async-start(), calls=%async_computation.9 | async-start | bytes 2359296 | tf_op jit(solution)/shard_map/all_gather | solution.py:54
  174.4 108.2 %all-gather.17.cloned.1.call-start = ((), (), s32[]{:S(2)}) async-start(), calls=%async_computation.13 | async-start | bytes 5242880 | tf_op jit(solution)/shard_map/all_gather | solution.py:78
  175.0 169.8 %all-gather.13.cloned.1.call-start = ((), (), s32[]{:S(2)}) async-start(), calls=%async_computation.11 | async-start | bytes 5242880 | tf_op jit(solution)/shard_map/all_gather | solution.py:76
  213.6 1.4 copy-start.5
  213.6 185.6 %all-gather.15.cloned.1.call-start = ((), (), s32[]{:S(2)}) async-start(), calls=%async_computation.12 | async-start | bytes 5242880 | tf_op jit(solution)/shard_map/all_gather | solution.py:77
  214.3 5.6 %copy-start.4 = (bf16[512,1024]{1,0:T(8,128)(2,1)S(1)}, bf16[512,1024]{1,0:T(8,128)(2,1)}, u32[]{:S(2)}) copy-start(bf16[512,1024]{1,0:T(8,128)(2,1)} %get-tuple-element.12) | copy-start | bytes 3145732
  214.4 234.0 %reduce-scatter.8.cloned.1.call-start = ((), (), s32[]{:S(2)}) async-start(), calls=%async_computation.10 | async-start | bytes 4718592 | tf_op jit(solution)/shard_map/reduce_scatter | solution.py:64
  214.9 5.0 %copy-start.9 = (bf16[2048,1024]{1,0:T(8,128)(2,1)S(1)}, bf16[2048,1024]{1,0:T(8,128)(2,1)}, u32[]{:S(2)}) copy-start(bf16[2048,1024]{1,0:T(8,128)(2,1)} %param.14) | copy-start | bytes 12582916
  224.3 1.6 copy-start.2
  227.4 50.2 %all-to-all-start.1 = ((bf16[512,4,512]{2,0,1:T(8,128)(2,1)}), bf16[512,4,512]{2,0,1:T(8,128)(2,1)S(1)}, u32[]{:S(2)}, u32[]{:S(2)}) async-start(bf16[512,4,512]{2,0,1:T(8,128)(2,1)} %bitcast.35), calls=%async_computation.4 | async-start | bytes 4194304 | tf_op jit(solution)/shard_map/all_to_all | solution.py:74
  277.6 38.8 %all-to-all-start = ((bf16[512,4,512]{2,0,1:T(8,128)(2,1)}), bf16[512,4,512]{2,0,1:T(8,128)(2,1)}, u32[]{:S(2)}, u32[]{:S(2)}) async-start(bf16[512,4,512]{2,0,1:T(8,128)(2,1)} %bitcast.36), calls=%async_computation.3 | async-start | bytes 4194304 | tf_op jit(solution)/shard_map/all_to_all | solution.py:73
  351.3 97.1 %copy-start = (bf16[64,2048]{1,0:T(8,128)(2,1)S(1)}, bf16[64,2048]{1,0:T(8,128)(2,1)}, u32[]{:S(2)}) copy-start(bf16[64,2048]{1,0:T(8,128)(2,1)} %param.10) | copy-start | bytes 786436
  351.3 97.1 %copy-start.7 = (f32[2048]{0:T(1024)S(1)}, f32[2048]{0:T(1024)}, u32[]{:S(2)}) copy-start(f32[2048]{0:T(1024)} %param.12) | copy-start | bytes 24580
Sparse Core Ops, SparseCore 0:
  10.4 30.2 all-gather.6
  42.9 28.5 all-gather.8
  73.7 46.1 reduce-scatter.3
  122.1 48.3 reduce-scatter.5
  174.5 30.7 all-gather.10
  207.0 72.2 all-gather.16
  281.1 63.6 all-gather.12
  346.6 52.5 all-gather.14
  401.5 46.7 reduce-scatter.7
where the time goes:
time: 502 us
  waiting for transfers between devices  348 us (69%)
  matrix products  70.1 us (14%)
  blocking collectives  43.4 us (9%)
  between operations  13.9 us (3%)
  other arithmetic  10.1 us (2%)
  starting transfers between devices  9.72 us (2%)
  local copies, waits for them, and re-layouts  6.77 us (1%)
    reduce_scatter x1, waiting for transfers between devices, local(): lax.psum_scatter(frozen_partial, 'tensor', scatter_dimension=0, tiled=True)  50.6 us
    all_gather x1, waiting for transfers between devices, local(): up_piece = lax.all_gather(up_grad, 'dp', axis=0, tiled=True)  48 us
    psum x1, blocking collectives, local(): grad_gain = lax.psum(gain_term, ('dp', 'tensor'))  43.4 us
    all_to_all x1, waiting for transfers between devices, local(): lax.all_to_all(grads_all, 'dp', split_axis=1, concat_axis=0, tiled=True)  42.9 us
    reduce_scatter x1, waiting for transfers between devices, local(): lax.psum_scatter(partial_normed, 'tensor', scatter_dimension=0, tiled=True)  42.6 us
    reduce_scatter x1, waiting for transfers between devices, local(): lax.psum_scatter(partial_learned, 'tensor', scatter_dimension=0, tiled=True)  30.8 us
    all_gather x1, waiting for transfers between devices, local(): grads_all = lax.all_gather(out_grad, 'tensor', axis=0, tiled=True)  30.1 us
    all_gather x1, waiting for transfers between devices, local(): lax.all_gather(normed, 'tensor', axis=0, tiled=True)  29.6 us
  transfers between devices with their start and end apart: 11, of which 10 were waited for; matrix products, arithmetic and copies ran while one was open for 15% of the time, Pallas kernels for 0%

commit v1 on v0

v1 whole, which is shorter than its diff:
```python
import math

import jax
import jax.numpy as jnp
from jax import lax
from jax.sharding import PartitionSpec as P

BF16 = jnp.bfloat16
F32 = jnp.float32


class Ring:
    def __init__(self, size):
        self.cores = 2 if size % 2 == 0 else 1
        self.nz = size // self.cores
        self.size = size

    def swap(self, x):
        return lax.ppermute(x, "tensor", [(i, i ^ 1) for i in range(self.size)])

    def shift(self, x, k):
        step = k * self.cores
        return lax.ppermute(x, "tensor", [(i, (i + step) % self.size) for i in range(self.size)])

    def gather(self, x):
        rows = x.shape[0]
        right, left, blocks = x, x, [x]
        for d in range(1, self.nz // 2 + 1):
            if 2 * d == self.nz:
                top = self.shift(right[: rows // 2], 1)
                bottom = self.shift(left[rows // 2 :], -1)
                blocks.append(jnp.concatenate([top, bottom], axis=0))
            else:
                right, left = self.shift(right, 1), self.shift(left, -1)
                blocks += [right, left]
        if self.cores == 1:
            return blocks
        out = []
        for b in blocks:
            out += [b, self.swap(b)]
        return out

    def scatter_sum(self, p):
        rows = p.shape[1]
        p = p.reshape((self.nz, self.cores) + p.shape[1:])
        q = p[:, 0]
        if self.cores == 2:
            q = q + self.swap(p[:, 1].astype(BF16)).astype(F32)
        dist = {0: 0}
        at = 1
        for d in range(1, self.nz // 2 + 1):
            dist[-d] = at
            dist[d] = at if 2 * d == self.nz else at + 1
            at = dist[d] + 1
        total = q[0]
        half = self.nz // 2
        if half == 0:
            return total
        top = q[dist[half]][: rows // 2]
        bottom = q[dist[half]][rows // 2 :]
        right = left = None
        if self.nz % 2 == 0:
            right, left = top, bottom
        for d in range(half - 1, 0, -1):
            r_in = self.shift(right.astype(BF16), 1).astype(F32)
            l_in = self.shift(left.astype(BF16), -1).astype(F32)
            if d == half - 1:
                zeros = jnp.zeros_like(r_in)
                r_in = jnp.concatenate([r_in, zeros], axis=0)
                l_in = jnp.concatenate([zeros, l_in], axis=0)
            right, left = q[dist[d]] + r_in, q[dist[-d]] + l_in
        r_in = self.shift(right.astype(BF16), 1).astype(F32)
        l_in = self.shift(left.astype(BF16), -1).astype(F32)
        if half == 1:
            return total + jnp.concatenate([r_in, l_in], axis=0)
        return total + r_in + l_in


class Grid:
    def __init__(self, size):
        self.a = 2 if size % 2 == 0 else 1
        self.b = size // self.a
        self.size = size

    def perm(self, x, da, db):
        a, b = self.a, self.b
        if da % a == 0 and db % b == 0:
            return x
        pairs = [
            (i * b + j, ((i + da) % a) * b + (j + db) % b) for i in range(a) for j in range(b)
        ]
        return lax.ppermute(x, "dp", pairs)


def everyone_sum(x, dp, tensor):
    for axis, size in (("tensor", tensor), ("dp", dp)):
        step = 1
        while step < size:
            x = x + lax.ppermute(x, axis, [(i, i ^ step) for i in range(size)])
            step *= 2
    return x


def project_up(normed, w_gate, w_up, w_down):
    gate_pre = jnp.dot(normed, w_gate, preferred_element_type=F32)
    up_pre = jnp.dot(normed, w_up, preferred_element_type=F32)
    hidden = (jax.nn.silu(gate_pre) * up_pre).astype(BF16)
    partial_out = jnp.dot(hidden, w_down, preferred_element_type=F32)
    return (gate_pre, up_pre, hidden, partial_out)


def tdot(x, y):
    return lax.dot_general(x, y, (((0,), (0,)), ((), ())), preferred_element_type=F32)


def make_local(dp, tensor):
    ring, grid = Ring(tensor), Grid(dp)
    a, b = grid.a, grid.b

    def own_core(x):
        return x.reshape((ring.nz, ring.cores, -1) + x.shape[1:])[:, 0].reshape((-1,) + x.shape[1:])

    def both_cores(x):
        if ring.cores == 1:
            return x
        mine = x.reshape((ring.nz, 1, -1) + x.shape[1:])
        other = ring.swap(x).reshape(mine.shape)
        return jnp.concatenate([mine, other], axis=1).reshape((-1,) + x.shape[1:])

    def local(
        tokens,
        targets,
        learner_gain,
        learner_gate,
        learner_up,
        learner_down,
        frozen_gain,
        frozen_gate,
        frozen_up,
        frozen_down,
    ):
        rows, width = tokens.shape
        cols = width // dp
        me = lax.axis_index("dp")
        ya, xb = me // b, me % b

        tokens_all = jnp.concatenate(ring.gather(tokens), axis=0)
        xall = tokens_all.astype(F32)
        inv_all = lax.rsqrt(jnp.mean(xall * xall, axis=-1, keepdims=True) + 1e-05)
        normed_all = (xall * inv_all * learner_gain).astype(BF16)
        frozen_all = (xall * inv_all * frozen_gain).astype(BF16)

        gate_pre, up_pre, hidden, partial_learned = project_up(
            normed_all, learner_gate, learner_up, learner_down
        )
        learned = ring.scatter_sum(partial_learned.reshape(-1, rows, width))
        frozen_partial = project_up(frozen_all, frozen_gate, frozen_up, frozen_down)[3]
        frozen_out = ring.scatter_sum(frozen_partial.reshape(-1, rows, width))

        def columns(x, ia, ib):
            return lax.dynamic_slice_in_dim(x, (ia * b + ib) * cols, cols, axis=1)

        half_normed = own_core(normed_all)
        fast_normed, slow_normed = [], []
        for s in range(b):
            src = normed_all if s == 0 else half_normed
            piece = jnp.concatenate(
                [columns(src, (ya + r) % a, (xb + s) % b) for r in range(a)], axis=1
            )
            fast_normed.append(piece if s == 0 else both_cores(grid.perm(piece, 0, s)))
        for s in range(a):
            src = normed_all if s == 0 else half_normed
            piece = jnp.concatenate(
                [columns(src, (ya + s) % a, (xb + r) % b) for r in range(b)], axis=1
            )
            slow_normed.append(piece if s == 0 else both_cores(grid.perm(piece, s, 0)))

        mid = hidden.shape[0] // 2
        top = [grid.perm(hidden[:mid], 0, s) for s in range(b)]
        top = {(r, s): grid.perm(top[s], r, 0) for s in range(b) for r in range(a)}
        bottom = [grid.perm(hidden[mid:], r, 0) for r in range(a)]
        bottom = {(r, s): grid.perm(bottom[r], 0, s) for s in range(b) for r in range(a)}

        goal = targets.astype(F32)
        root = math.sqrt(width)
        miss = learned - goal
        frozen_miss = frozen_out - goal
        learner_loss = 0.5 * jnp.sum(miss * miss, axis=-1) / root
        frozen_loss = 0.5 * jnp.sum(frozen_miss * frozen_miss, axis=-1) / root
        scores = learner_loss - frozen_loss
        weight = jax.nn.sigmoid(scores)
        out_grad = (weight[:, None] * miss / root).astype(BF16)
        grads_all = jnp.concatenate(ring.gather(out_grad), axis=0)

        hidden_grad = jnp.dot(grads_all, learner_down.T, preferred_element_type=F32)
        sigma = jax.nn.sigmoid(gate_pre)
        gate_grad = (hidden_grad * up_pre * sigma * (1.0 + gate_pre * (1.0 - sigma))).astype(BF16)
        up_grad = (hidden_grad * gate_pre * sigma).astype(BF16)

        half_grads = own_core(grads_all)
        grad_cols = {}
        for r in range(a):
            for s in range(b):
                if r == 0 and s == 0:
                    grad_cols[r, s] = columns(grads_all, ya, xb)
                else:
                    piece = columns(half_grads, (ya + r) % a, (xb + s) % b)
                    grad_cols[r, s] = both_cores(grid.perm(piece, r, s))

        gate_parts = [grid.perm(gate_grad, 0, s) for s in range(b)]
        up_parts = [grid.perm(up_grad, s, 0) for s in range(a)]

        partial_normed = jnp.dot(
            gate_grad, learner_gate.T, preferred_element_type=F32
        ) + jnp.dot(up_grad, learner_up.T, preferred_element_type=F32)
        normed_grad = ring.scatter_sum(partial_normed.reshape(-1, rows, width))

        hidden_set = jnp.concatenate(
            [h for key in grad_cols for h in (top[key], bottom[key])], axis=0
        )
        cols_set = jnp.concatenate([grad_cols[key] for key in grad_cols], axis=0)
        grad_down = tdot(hidden_set, cols_set)

        def outer(normed_parts, grad_parts, r):
            span = slice(r * cols, (r + 1) * cols)
            return sum(tdot(n[:, span], g) for n, g in zip(normed_parts, grad_parts))

        grad_gate = outer(fast_normed, gate_parts, 0)
        for r in range(1, a):
            term = outer(fast_normed, gate_parts, r).astype(BF16)
            grad_gate = grad_gate + grid.perm(term, r, 0).astype(F32)
        grad_up = outer(slow_normed, up_parts, 0)
        for r in range(1, b):
            term = outer(slow_normed, up_parts, r).astype(BF16)
            grad_up = grad_up + grid.perm(term, 0, r).astype(F32)

        xfloat = tokens.astype(F32)
        inv_rms = lax.rsqrt(jnp.mean(xfloat * xfloat, axis=-1, keepdims=True) + 1e-05)
        gain_term = jnp.sum(normed_grad * xfloat * inv_rms, axis=0)
        grad_gain = everyone_sum(gain_term, dp, tensor)
        scaled = learner_gain * normed_grad
        cubed = inv_rms * inv_rms * inv_rms
        grad_tokens = (
            inv_rms * scaled - xfloat * cubed * jnp.mean(scaled * xfloat, axis=-1, keepdims=True)
        ).astype(BF16)
        return (scores, grad_tokens, grad_gain, grad_gate, grad_up, grad_down)

    return local


def solution(mesh):
    placed = (
        P(("dp", "tensor"), None),
        P(("dp", "tensor"), None),
        P(),
        P(None, "tensor"),
        P(None, "tensor"),
        P("tensor", None),
        P(),
        P(None, "tensor"),
        P(None, "tensor"),
        P("tensor", None),
    )
    return jax.shard_map(
        make_local(mesh.shape["dp"], mesh.shape["tensor"]),
        mesh=mesh,
        in_specs=placed,
        out_specs=(
            P(("dp", "tensor")),
            P(("dp", "tensor"), None),
            P(),
            P("dp", "tensor"),
            P("dp", "tensor"),
            P("tensor", "dp"),
        ),
        check_vma=False,
    )
```

time: 502 us -> 250 us (0.50)
  waiting for transfers between devices: 348 us -> 134 us
  blocking collectives: 43.4 us -> 0 us
  starting transfers between devices: 9.72 us -> 45.8 us
  matrix products: 70.1 us -> 40.8 us
  between operations: 13.9 us -> 1.46 us
  local copies, waits for them, and re-layouts: 6.77 us -> 15.1 us
    all_gather x6 -> x0, waiting for transfers between devices: 151 us -> none  [the longest x1 48 us: local(): up_piece = lax.all_gather(up_grad, 'dp', axis=0, tiled=True)]
    ppermute x0 -> x56, waiting for transfers between devices: none -> 134 us  [the longest x20 75.5 us: shift(): lax.ppermute(x, 'tensor', [(i, (i + step) % self.size) for i in range(sel...]
    reduce_scatter x3 -> x0, waiting for transfers between devices: 124 us -> none  [the longest x1 50.6 us: local(): lax.psum_scatter(frozen_partial, 'tensor', scatter_dimension=0, tiled=True)]
    all_to_all x2 -> x0, waiting for transfers between devices: 70.9 us -> none  [the longest x1 42.9 us: local(): lax.all_to_all(grads_all, 'dp', split_axis=1, concat_axis=0, tiled=True)]
    ppermute x0 -> x56, starting transfers between devices: none -> 45.8 us  [the longest x20 23.5 us: shift(): lax.ppermute(x, 'tensor', [(i, (i + step) % self.size) for i in range(sel...]
    psum x1 -> x0, blocking collectives: 43.4 us -> none  [local(): grad_gain = lax.psum(gain_term, ('dp', 'tensor'))]
    dot_general x11 -> x17, matrix products: 70.1 us -> 40.8 us  [the longest x2 13.2 us: project_up(): partial_out = jnp.dot(hidden, w_down, preferred_element_type=F32)]
    all_to_all x2 -> x0, starting transfers between devices: 9.18 us -> none  [the longest x1 4.98 us: local(): lax.all_to_all(normed_all, 'dp', split_axis=1, concat_axis=0, tiled=True)]
  transfers between devices with their start and end apart: 11 -> 56, of which waited for: 10 -> 28; matrix products, arithmetic and copies ran while one was open for 15% -> 19% of each run, Pallas kernels for 0% -> 0%
where the time goes in v1:
time: 250 us; the launch traced here: 249 us
  waiting for transfers between devices  134 us (54%)
  starting transfers between devices  45.8 us (18%)
  matrix products  40.8 us (16%)
  local copies, waits for them, and re-layouts  15.1 us (6%)
  other arithmetic  11.8 us (5%)
    ppermute x20, waiting for transfers between devices, shift(): lax.ppermute(x, 'tensor', [(i, (i + step) % self.size) for i in range(sel...  75.5 us
    ppermute x15, waiting for transfers between devices, perm(): return lax.ppermute(x, 'dp', pairs)  31.4 us
    ppermute x20, starting transfers between devices, shift(): lax.ppermute(x, 'tensor', [(i, (i + step) % self.size) for i in range(sel...  23.5 us
    ppermute x5, waiting for transfers between devices, everyone_sum(): x = x + lax.ppermute(x, axis, [(i, i ^ step) for i in range(size)])  23.2 us
    ppermute x15, starting transfers between devices, perm(): return lax.ppermute(x, 'dp', pairs)  17.9 us
    dot_general x2, matrix products, project_up(): partial_out = jnp.dot(hidden, w_down, preferred_element_type=F32)  13.2 us
    unnamed x56, local copies, waits for them, and re-layouts  11.3 us
    dot_general x9, matrix products, tdot(): lax.dot_general(x, y, (((0,), (0,)), ((), ())), preferred_element_type=F32)  9.62 us
  transfers between devices with their start and end apart: 56, of which 28 were waited for; matrix products, arithmetic and copies ran while one was open for 19% of the time, Pallas kernels for 0%

profile of v1, /device:TPU:12, one launch (start us, length us, event | category | flops | bytes accessed | tf_op | source)
XLA Modules:
  0.0 248.6 jit_solution(3768606328156355450)
XLA Ops:
  1.1 1.6 collective-permute-start.1
  4.9 4.1 %collective-permute-done.3 = bf16[64,2048]{1,0:T(8,128)(2,1)S(1)} collective-permute-done((bf16[64,2048]{1,0:T(8,128)(2,1)}, bf16[64,2048]{1,0:T(8,128)(2,1)S(1)}, u32[]{:S(2)}, u32[]{:S(2)}) %collective-permute-start.3) | collective-permute-done | bytes 262176 | tf_op jit(solution)/shard_map/ppermute | solution.py:23
  9.1 2.7 %collective-permute-start.6 = (bf16[32,2048]{1,0:T(8,128)(2,1)S(1)}, bf16[32,2048]{1,0:T(8,128)(2,1)S(1)}, u32[]{:S(2)}, u32[]{:S(2)}) collective-permute-start(bf16[32,2048]{1,0:T(8,128)(2,1)S(1)} %slice.163), channel_id=1, source_target_pairs={{0,6},{1,7},{2,0},{3,1},{4,2},{5,3},{6,4},{7,5},{8,14},{9,15},{10,... | collective-permute-start | bytes 393224 | tf_op jit(solution)/shard_map/ppermute | solution.py:23
  11.8 5.9 %collective-permute-done.1 = bf16[64,2048]{1,0:T(8,128)(2,1)S(1)} collective-permute-done((bf16[64,2048]{1,0:T(8,128)(2,1)}, bf16[64,2048]{1,0:T(8,128)(2,1)S(1)}, u32[]{:S(2)}, u32[]{:S(2)}) %collective-permute-start.1) | collective-permute-done | bytes 262176 | tf_op jit(solution)/shard_map/ppermute | solution.py:23
  18.4 4.3 %collective-permute-done.5 = bf16[32,2048]{1,0:T(8,128)(2,1)S(1)} collective-permute-done((bf16[32,2048]{1,0:T(8,128)(2,1)S(1)}, bf16[32,2048]{1,0:T(8,128)(2,1)S(1)}, u32[]{:S(2)}, u32[]{:S(2)}) %collective-permute-start.5) | collective-permute-done | bytes 131104 | tf_op jit(solution)/shard_map/ppermute | solution.py:23
  25.5 1.6 copy-done.9
  27.2 2.3 fusion.78
  30.1 4.1 %constant_dynamic-update-slice_fusion.24 = (bf16[2048,1024]{1,0:T(8,128)(2,1)}, bf16[512,1024]{1,0:T(8,128)(2,1)S(1)}, f32[512,1024]{1,0:T(8,128)}) fusion(f32[512,1024]{1,0:T(8,128)S(1)} %fusion.78, bf16[512,2048]{1,0:T(8,128)(2,1)S(1)} %multiply_convert_fusion.1, bf16[2048,1024]{1,0:T(8,128)(2,1)S(1)} %copy-done.11), kind=kOutput, calls=%fused_computation.137 | convolution fusion | flops 2150629376 | bytes 12582912 | tf_op jit(solution)/shard_map/dot_general | solution.py:106
  39.4 3.8 %fusion.17 = f32[512,1024]{1,0:T(8,128)} fusion(bf16[2048,1024]{1,0:T(8,128)(2,1)S(1)} %copy-done.7, bf16[512,2048]{1,0:T(8,128)(2,1)S(1)} %constant_dynamic-update-slice_fusion, f32[2048]{0:T(1024)S(1)} %copy-done.14, f32[512]{0:T(512)S(1)} %add_rsqrt_fusion), kind=kOutput, calls=%fused_computation.45 | convolution fusion | flops 2151677952 | bytes 8398848 | tf_op jit(solution)/shard_map/dot_general | solution.py:105
  43.2 10.7 %fusion.16 = f32[512,2048]{1,0:T(8,128)} fusion(bf16[1024,2048]{1,0:T(8,128)(2,1)} %param.19, f32[512,1024]{1,0:T(8,128)} %fusion.17, bf16[2048,1024]{1,0:T(8,128)(2,1)} %param.18, bf16[512,2048]{1,0:T(8,128)(2,1)S(1)} %constant_dynamic-update-slice_fusion, f32[2048]{0:T(1024)S(1)} %copy-done.14, f32[512]{0:T(512)S(1)} %add_rsqrt_fusion), kind=kOutput, calls=%fused_computation.42 | convolution fusion | flops 4302307328 | bytes 16787456 | tf_op jit(solution)/shard_map/dot_general | solution.py:108
  53.8 1.7 fusion.14
  56.7 1.8 copy-done.8
  58.5 2.6 %fusion.79 = f32[512,2048]{1,0:T(8,128)S(1)} fusion(bf16[512,1024]{1,0:T(8,128)(2,1)S(1)} %get-tuple-element.11, bf16[1024,2048]{1,0:T(8,128)(2,1)S(1)} %copy-done.8), kind=kOutput, calls=%fused_computation.162 | convolution fusion | flops 2147483648 | bytes 9437184 | tf_op jit(solution)/shard_map/dot_general | solution.py:108
  67.8 7.7 %collective-permute-done.40 = bf16[256,1024]{1,0:T(8,128)(2,1)S(1)} collective-permute-done((bf16[256,1024]{1,0:T(8,128)(2,1)S(1)}, bf16[256,1024]{1,0:T(8,128)(2,1)S(1)}, u32[]{:S(2)}, u32[]{:S(2)}) %collective-permute-start.40) | collective-permute-done | bytes 524320 | tf_op jit(solution)/shard_map/ppermute | solution.py:92
  78.4 1.7 collective-permute-start.16
  80.6 3.6 %collective-permute-done.14 = bf16[32,2048]{1,0:T(8,128)(2,1)S(1)} collective-permute-done((bf16[32,2048]{1,0:T(8,128)(2,1)S(1)}, bf16[32,2048]{1,0:T(8,128)(2,1)S(1)}, u32[]{:S(2)}, u32[]{:S(2)}) %collective-permute-start.14) | collective-permute-done | bytes 131104 | tf_op jit(solution)/shard_map/ppermute | solution.py:23
  84.3 2.5 %collective-permute-done.16 = bf16[32,2048]{1,0:T(8,128)(2,1)S(1)} collective-permute-done((bf16[32,2048]{1,0:T(8,128)(2,1)S(1)}, bf16[32,2048]{1,0:T(8,128)(2,1)S(1)}, u32[]{:S(2)}, u32[]{:S(2)}) %collective-permute-start.16) | collective-permute-done | bytes 131104 | tf_op jit(solution)/shard_map/ppermute | solution.py:23
  86.9 2.0 collective-permute-start.11
  88.9 2.3 collective-permute-done.9
  91.7 4.1 %collective-permute-done.11 = bf16[32,2048]{1,0:T(8,128)(2,1)S(1)} collective-permute-done((bf16[32,2048]{1,0:T(8,128)(2,1)S(1)}, bf16[32,2048]{1,0:T(8,128)(2,1)S(1)}, u32[]{:S(2)}, u32[]{:S(2)}) %collective-permute-start.11) | collective-permute-done | bytes 131104 | tf_op jit(solution)/shard_map/ppermute | solution.py:23
  98.0 2.2 collective-permute-start.12
  100.3 1.6 collective-permute-start.49
  103.2 7.4 %collective-permute-done.17 = bf16[64,2048]{1,0:T(8,128)(2,1)S(1)} collective-permute-done((bf16[64,2048]{1,0:T(8,128)(2,1)S(1)}, bf16[64,2048]{1,0:T(8,128)(2,1)S(1)}, u32[]{:S(2)}, u32[]{:S(2)}) %collective-permute-start.17) | collective-permute-done | bytes 262176 | tf_op jit(solution)/shard_map/ppermute | solution.py:23
  110.6 3.9 %collective-permute-done.10 = bf16[64,2048]{1,0:T(8,128)(2,1)S(1)} collective-permute-done((bf16[64,2048]{1,0:T(8,128)(2,1)S(1)}, bf16[64,2048]{1,0:T(8,128)(2,1)S(1)}, u32[]{:S(2)}, u32[]{:S(2)}) %collective-permute-start.10) | collective-permute-done | bytes 262176 | tf_op jit(solution)/shard_map/ppermute | solution.py:23
  114.5 4.1 %collective-permute-done.12 = bf16[64,2048]{1,0:T(8,128)(2,1)S(1)} collective-permute-done((bf16[64,2048]{1,0:T(8,128)(2,1)S(1)}, bf16[64,2048]{1,0:T(8,128)(2,1)S(1)}, u32[]{:S(2)}, u32[]{:S(2)}) %collective-permute-start.12) | collective-permute-done | bytes 262176 | tf_op jit(solution)/shard_map/ppermute | solution.py:23
  121.9 11.7 %collective-permute-done.21 = bf16[64,2048]{1,0:T(8,128)(2,1)S(1)} collective-permute-done((bf16[64,2048]{1,0:T(8,128)(2,1)S(1)}, bf16[64,2048]{1,0:T(8,128)(2,1)S(1)}, u32[]{:S(2)}, u32[]{:S(2)}) %collective-permute-start.21) | collective-permute-done | bytes 262176 | tf_op jit(solution)/shard_map/ppermute | solution.py:23
  134.1 1.6 collective-permute-start.23
  136.3 2.7 %collective-permute-done.24 = bf16[32,2048]{1,0:T(8,128)(2,1)S(1)} collective-permute-done((bf16[32,2048]{1,0:T(8,128)(2,1)S(1)}, bf16[32,2048]{1,0:T(8,128)(2,1)S(1)}, u32[]{:S(2)}, u32[]{:S(2)}) %collective-permute-start.24) | collective-permute-done | bytes 131104 | tf_op jit(solution)/shard_map/ppermute | solution.py:23
  140.8 3.0 %multiply_convert_fusion.2 = (bf16[512,1024]{1,0:T(8,128)(2,1)S(1)}, bf16[512,1024]{1,0:T(8,128)(2,1)S(1)}) fusion(f32[512,1024]{1,0:T(8,128)S(1)} %copy-done.16, f32[512,1024]{1,0:T(8,128)S(1)} %copy-done.17, bf16[512,2048]{1,0:T(8,128)(2,1)S(1)} %constant_dynamic-update-slice_fusion.9, bf16[1024,2048]{1,0:T(8,128)(2,1)S(1)} %copy-done.8), kind=kOutput, calls=%fused_computation.28 | convolution fusion | flops 2154299392 | bytes 12582912 | tf_op jit(solution)/shard_map/dot_general | solution.py:195
  143.8 1.6 collective-permute-start.38
  145.3 2.4 fusion.80
  148.5 2.5 collective-permute-start.54
  153.0 2.4 convolution_add_fusion
  157.7 17.8 %collective-permute-done.50 = bf16[256,512]{1,0:T(8,128)(2,1)S(1)} collective-permute-done((bf16[256,512]{1,0:T(8,128)(2,1)S(1)}, bf16[256,512]{1,0:T(8,128)(2,1)S(1)}, u32[]{:S(2)}, u32[]{:S(2)}) %collective-permute-start.50) | collective-permute-done | bytes 262176 | tf_op jit(solution)/shard_map/ppermute | solution.py:92
  175.5 5.8 %collective-permute-done.54 = bf16[256,512]{1,0:T(8,128)(2,1)S(1)} collective-permute-done((bf16[256,512]{1,0:T(8,128)(2,1)S(1)}, bf16[256,512]{1,0:T(8,128)(2,1)S(1)}, u32[]{:S(2)}, u32[]{:S(2)}) %collective-permute-start.54) | collective-permute-done | bytes 262176 | tf_op jit(solution)/shard_map/ppermute | solution.py:92
  183.9 3.7 %fusion.5 = f32[1024,512]{1,0:T(8,128)} fusion(bf16[2048,1024]{1,0:T(8,128)(2,1)S(1)} %constant_dynamic-update-slice_fusion.18, bf16[512,512]{1,0:T(8,128)(2,1)S(1)} %bitcast.164, bf16[512,512]{1,0:T(8,128)(2,1)S(1)} %bitcast.165, bf16[512,512]{1,0:T(8,128)(2,1)S(1)} %bitcast.163, bf16[512,512]{1,0:T(8,128)(2,1)S(1)} %constant_dynamic-slice_fusion.3), kind=kOutput, calls=%fused_computation.16 | convolution fusion | flops 2155872256 | bytes 8388608 | tf_op jit(solution)/shard_map/dot_general | solution.py:113
  188.1 2.4 collective-permute-start.27
  193.2 1.7 collective-permute-done.27
  194.8 3.9 %collective-permute-done.29 = bf16[32,2048]{1,0:T(8,128)(2,1)S(1)} collective-permute-done((bf16[32,2048]{1,0:T(8,128)(2,1)S(1)}, bf16[32,2048]{1,0:T(8,128)(2,1)S(1)}, u32[]{:S(2)}, u32[]{:S(2)}) %collective-permute-start.29) | collective-permute-done | bytes 131104 | tf_op jit(solution)/shard_map/ppermute | solution.py:23
  198.8 1.6 collective-permute-start.28
  201.7 9.7 %collective-permute-done.28 = bf16[64,2048]{1,0:T(8,128)(2,1)S(1)} collective-permute-done((bf16[64,2048]{1,0:T(8,128)(2,1)S(1)}, bf16[64,2048]{1,0:T(8,128)(2,1)S(1)}, u32[]{:S(2)}, u32[]{:S(2)}) %collective-permute-start.28) | collective-permute-done | bytes 262176 | tf_op jit(solution)/shard_map/ppermute | solution.py:23
  211.4 2.1 collective-permute-done.30
  217.3 2.6 %collective-permute-done.32 = f32[2048]{0:T(1024)S(1)} collective-permute-done((f32[2048]{0:T(1024)S(1)}, f32[2048]{0:T(1024)S(1)}, u32[]{:S(2)}, u32[]{:S(2)}) %collective-permute-start.32) | collective-permute-done | bytes 8224 | tf_op jit(solution)/shard_map/ppermute | solution.py:99
  221.5 2.9 %collective-permute-done.33 = f32[2048]{0:T(1024)S(1)} collective-permute-done((f32[2048]{0:T(1024)S(1)}, f32[2048]{0:T(1024)S(1)}, u32[]{:S(2)}, u32[]{:S(2)}) %collective-permute-start.33) | collective-permute-done | bytes 8224 | tf_op jit(solution)/shard_map/ppermute | solution.py:99
  225.0 15.5 %collective-permute-done.34 = f32[2048]{0:T(1024)S(1)} collective-permute-done((f32[2048]{0:T(1024)S(1)}, f32[2048]{0:T(1024)S(1)}, u32[]{:S(2)}, u32[]{:S(2)}) %collective-permute-start.34) | collective-permute-done | bytes 8224 | tf_op jit(solution)/shard_map/ppermute | solution.py:99
  241.9 2.2 collective-permute-done.35
  244.7 1.9 convert_add_fusion
  246.6 1.9 convert_add_fusion.1
  (192 shorter events, 53.4 us)
Async XLA Ops:
  0.6 8.4 %collective-permute-start.3 = (bf16[64,2048]{1,0:T(8,128)(2,1)}, bf16[64,2048]{1,0:T(8,128)(2,1)S(1)}, u32[]{:S(2)}, u32[]{:S(2)}) collective-permute-start(bf16[64,2048]{1,0:T(8,128)(2,1)} %param.10), channel_id=1, source_target_pairs={{0,6},{1,7},{2,0},{3,1},{4,2},{5,3},{6,4},{7,5},{8,14},{9,15},{10,... | collective-permute-start | bytes 786440 | tf_op jit(solution)/shard_map/ppermute | solution.py:23
  1.1 16.6 %collective-permute-start.1 = (bf16[64,2048]{1,0:T(8,128)(2,1)}, bf16[64,2048]{1,0:T(8,128)(2,1)S(1)}, u32[]{:S(2)}, u32[]{:S(2)}) collective-permute-start(bf16[64,2048]{1,0:T(8,128)(2,1)} %param.10), channel_id=1, source_target_pairs={{0,2},{1,3},{2,4},{3,5},{4,6},{5,7},{6,0},{7,1},{8,10},{9,11},{10,... | collective-permute-start | bytes 786440 | tf_op jit(solution)/shard_map/ppermute | solution.py:23
  2.7 15.7 %collective-permute-start = (bf16[64,2048]{1,0:T(8,128)(2,1)}, bf16[64,2048]{1,0:T(8,128)(2,1)S(1)}, u32[]{:S(2)}, u32[]{:S(2)}) collective-permute-start(bf16[64,2048]{1,0:T(8,128)(2,1)} %param.10), channel_id=1, source_target_pairs={{0,1},{1,0},{2,3},{3,2},{4,5},{5,4},{6,7},{7,6},{8,9},{9,8},{10,11... | collective-permute-start | bytes 786440 | tf_op jit(solution)/shard_map/ppermute | solution.py:19
  9.1 9.4 %collective-permute-start.6 = (bf16[32,2048]{1,0:T(8,128)(2,1)S(1)}, bf16[32,2048]{1,0:T(8,128)(2,1)S(1)}, u32[]{:S(2)}, u32[]{:S(2)}) collective-permute-start(bf16[32,2048]{1,0:T(8,128)(2,1)S(1)} %slice.163), channel_id=1, source_target_pairs={{0,6},{1,7},{2,0},{3,1},{4,2},{5,3},{6,4},{7,5},{8,14},{9,15},{10,... | collective-permute-start | bytes 393224 | tf_op jit(solution)/shard_map/ppermute | solution.py:23
  17.7 5.0 %collective-permute-start.5 = (bf16[32,2048]{1,0:T(8,128)(2,1)S(1)}, bf16[32,2048]{1,0:T(8,128)(2,1)S(1)}, u32[]{:S(2)}, u32[]{:S(2)}) collective-permute-start(bf16[32,2048]{1,0:T(8,128)(2,1)S(1)} %slice.162), channel_id=1, source_target_pairs={{0,2},{1,3},{2,4},{3,5},{4,6},{5,7},{6,0},{7,1},{8,10},{9,11},{10,... | collective-permute-start | bytes 393224 | tf_op jit(solution)/shard_map/ppermute | solution.py:23
  17.8 5.1 %collective-permute-start.4 = (bf16[64,2048]{1,0:T(8,128)(2,1)S(1)}, bf16[64,2048]{1,0:T(8,128)(2,1)S(1)}, u32[]{:S(2)}, u32[]{:S(2)}) collective-permute-start(bf16[64,2048]{1,0:T(8,128)(2,1)S(1)} %collective-permute-done.3), channel_id=1, source_target_pairs={{0,1},{1,0},{2,3},{3,2},{4,5},{5,4},{6,7},{7,6},{8,9},{9,8},{10,11... | collective-permute-start | bytes 786440 | tf_op jit(solution)/shard_map/ppermute | solution.py:19
  17.9 5.0 %collective-permute-start.2 = (bf16[64,2048]{1,0:T(8,128)(2,1)S(1)}, bf16[64,2048]{1,0:T(8,128)(2,1)S(1)}, u32[]{:S(2)}, u32[]{:S(2)}) collective-permute-start(bf16[64,2048]{1,0:T(8,128)(2,1)S(1)} %collective-permute-done.1), channel_id=1, source_target_pairs={{0,1},{1,0},{2,3},{3,2},{4,5},{5,4},{6,7},{7,6},{8,9},{9,8},{10,11... | collective-permute-start | bytes 786440 | tf_op jit(solution)/shard_map/ppermute | solution.py:19
  35.4 40.7 %collective-permute-start.47 = (bf16[256,1024]{1,0:T(8,128)(2,1)}, bf16[256,1024]{1,0:T(8,128)(2,1)}, u32[]{:S(2)}, u32[]{:S(2)}) collective-permute-start(bf16[256,1024]{1,0:T(8,128)(2,1)} %get-tuple-element.33), channel_id=1, source_target_pairs={{0,16},{8,24},{16,0},{24,8},{1,17},{9,25},{17,1},{25,9},{2,18},{10... | collective-permute-start | bytes 1572872 | tf_op jit(solution)/shard_map/ppermute | solution.py:92
  35.9 28.2 %collective-permute-start.45 = (bf16[256,1024]{1,0:T(8,128)(2,1)}, bf16[256,1024]{1,0:T(8,128)(2,1)}, u32[]{:S(2)}, u32[]{:S(2)}) collective-permute-start(bf16[256,1024]{1,0:T(8,128)(2,1)} %get-tuple-element.33), channel_id=1, source_target_pairs={{0,8},{8,0},{16,24},{24,16},{1,9},{9,1},{17,25},{25,17},{2,10},{10... | collective-permute-start | bytes 1572872 | tf_op jit(solution)/shard_map/ppermute | solution.py:92
  37.4 29.3 %collective-permute-start.46 = (bf16[256,1024]{1,0:T(8,128)(2,1)}, bf16[256,1024]{1,0:T(8,128)(2,1)}, u32[]{:S(2)}, u32[]{:S(2)}) collective-permute-start(bf16[256,1024]{1,0:T(8,128)(2,1)} %get-tuple-element.34), channel_id=1, source_target_pairs={{0,16},{8,24},{16,0},{24,8},{1,17},{9,25},{17,1},{25,9},{2,18},{10... | collective-permute-start | bytes 1572872 | tf_op jit(solution)/shard_map/ppermute | solution.py:92
  38.9 22.3 %collective-permute-start.44 = (bf16[256,1024]{1,0:T(8,128)(2,1)}, bf16[256,1024]{1,0:T(8,128)(2,1)}, u32[]{:S(2)}, u32[]{:S(2)}) collective-permute-start(bf16[256,1024]{1,0:T(8,128)(2,1)} %get-tuple-element.34), channel_id=1, source_target_pairs={{0,8},{8,0},{16,24},{24,16},{1,9},{9,1},{17,25},{25,17},{2,10},{10... | collective-permute-start | bytes 1572872 | tf_op jit(solution)/shard_map/ppermute | solution.py:92
  55.6 21.6 %collective-permute-start.13 = (bf16[4,64,2048]{2,1,0:T(8,128)(2,1)S(1)}, bf16[4,64,2048]{2,1,0:T(8,128)(2,1)S(1)}, u32[]{:S(2)}, u32[]{:S(2)}) collective-permute-start(bf16[4,64,2048]{2,1,0:T(8,128)(2,1)S(1)} %fusion.14), channel_id=1, source_target_pairs={{0,1},{1,0},{2,3},{3,2},{4,5},{5,4},{6,7},{7,6},{8,9},{9,8},{10,11... | collective-permute-start | bytes 3145736 | tf_op jit(solution)/shard_map/ppermute | solution.py:19
  61.2 14.4 %collective-permute-start.40 = (bf16[256,1024]{1,0:T(8,128)(2,1)S(1)}, bf16[256,1024]{1,0:T(8,128)(2,1)S(1)}, u32[]{:S(2)}, u32[]{:S(2)}) collective-permute-start(bf16[256,1024]{1,0:T(8,128)(2,1)S(1)} %get-tuple-element.44), channel_id=1, source_target_pairs={{0,16},{8,24},{16,0},{24,8},{1,17},{9,25},{17,1},{25,9},{2,18},{10... | collective-permute-start | bytes 1572872 | tf_op jit(solution)/shard_map/ppermute | solution.py:92
  64.0 36.2 %collective-permute-start.36 = (bf16[256,1024]{1,0:T(8,128)(2,1)S(1)}, bf16[256,1024]{1,0:T(8,128)(2,1)S(1)}, u32[]{:S(2)}, u32[]{:S(2)}) collective-permute-start(bf16[256,1024]{1,0:T(8,128)(2,1)S(1)} %get-tuple-element.45), channel_id=1, source_target_pairs={{0,8},{8,0},{16,24},{24,16},{1,9},{9,1},{17,25},{25,17},{2,10},{10... | collective-permute-start | bytes 1572872 | tf_op jit(solution)/shard_map/ppermute | solution.py:92
  66.7 11.7 %collective-permute-start.8 = (bf16[4,64,2048]{2,1,0:T(8,128)(2,1)S(1)}, bf16[4,64,2048]{2,1,0:T(8,128)(2,1)S(1)}, u32[]{:S(2)}, u32[]{:S(2)}) collective-permute-start(bf16[4,64,2048]{2,1,0:T(8,128)(2,1)S(1)} %fusion.13), channel_id=1, source_target_pairs={{0,1},{1,0},{2,3},{3,2},{4,5},{5,4},{6,7},{7,6},{8,9},{9,8},{10,11... | collective-permute-start | bytes 3145736 | tf_op jit(solution)/shard_map/ppermute | solution.py:19
  75.6 22.4 %collective-permute-start.48 = (bf16[256,1024]{1,0:T(8,128)(2,1)}, bf16[256,1024]{1,0:T(8,128)(2,1)S(1)}, u32[]{:S(2)}, u32[]{:S(2)}) collective-permute-start(bf16[256,1024]{1,0:T(8,128)(2,1)} %collective-permute-done.44), channel_id=1, source_target_pairs={{0,16},{8,24},{16,0},{24,8},{1,17},{9,25},{17,1},{25,9},{2,18},{10... | collective-permute-start | bytes 1572872 | tf_op jit(solution)/shard_map/ppermute | solution.py:92
  76.1 20.7 %collective-permute-start.41 = (bf16[256,1024]{1,0:T(8,128)(2,1)S(1)}, bf16[256,1024]{1,0:T(8,128)(2,1)S(1)}, u32[]{:S(2)}, u32[]{:S(2)}) collective-permute-start(bf16[256,1024]{1,0:T(8,128)(2,1)S(1)} %collective-permute-done.40), channel_id=1, source_target_pairs={{0,1},{1,0},{2,3},{3,2},{4,5},{5,4},{6,7},{7,6},{8,9},{9,8},{10,11... | collective-permute-start | bytes 1572872 | tf_op jit(solution)/shard_map/ppermute | solution.py:19
  77.7 6.5 %collective-permute-start.14 = (bf16[32,2048]{1,0:T(8,128)(2,1)S(1)}, bf16[32,2048]{1,0:T(8,128)(2,1)S(1)}, u32[]{:S(2)}, u32[]{:S(2)}) collective-permute-start(bf16[32,2048]{1,0:T(8,128)(2,1)S(1)} %get-tuple-element.40), channel_id=1, source_target_pairs={{0,2},{1,3},{2,4},{3,5},{4,6},{5,7},{6,0},{7,1},{8,10},{9,11},{10,... | collective-permute-start | bytes 393224 | tf_op jit(solution)/shard_map/ppermute | solution.py:23
  78.4 8.4 %collective-permute-start.16 = (bf16[32,2048]{1,0:T(8,128)(2,1)S(1)}, bf16[32,2048]{1,0:T(8,128)(2,1)S(1)}, u32[]{:S(2)}, u32[]{:S(2)}) collective-permute-start(bf16[32,2048]{1,0:T(8,128)(2,1)S(1)} %get-tuple-element.41), channel_id=1, source_target_pairs={{0,6},{1,7},{2,0},{3,1},{4,2},{5,3},{6,4},{7,5},{8,14},{9,15},{10,... | collective-permute-start | bytes 393224 | tf_op jit(solution)/shard_map/ppermute | solution.py:23
  84.2 7.0 %collective-permute-start.9 = (bf16[32,2048]{1,0:T(8,128)(2,1)S(1)}, bf16[32,2048]{1,0:T(8,128)(2,1)S(1)}, u32[]{:S(2)}, u32[]{:S(2)}) collective-permute-start(bf16[32,2048]{1,0:T(8,128)(2,1)S(1)} %get-tuple-element.42), channel_id=1, source_target_pairs={{0,2},{1,3},{2,4},{3,5},{4,6},{5,7},{6,0},{7,1},{8,10},{9,11},{10,... | collective-permute-start | bytes 393224 | tf_op jit(solution)/shard_map/ppermute | solution.py:23
  86.9 8.9 %collective-permute-start.11 = (bf16[32,2048]{1,0:T(8,128)(2,1)S(1)}, bf16[32,2048]{1,0:T(8,128)(2,1)S(1)}, u32[]{:S(2)}, u32[]{:S(2)}) collective-permute-start(bf16[32,2048]{1,0:T(8,128)(2,1)S(1)} %get-tuple-element.43), channel_id=1, source_target_pairs={{0,6},{1,7},{2,0},{3,1},{4,2},{5,3},{6,4},{7,5},{8,14},{9,15},{10,... | collective-permute-start | bytes 393224 | tf_op jit(solution)/shard_map/ppermute | solution.py:23
  91.2 12.0 %collective-permute-start.15 = (bf16[64,2048]{1,0:T(8,128)(2,1)S(1)}, bf16[64,2048]{1,0:T(8,128)(2,1)S(1)}, u32[]{:S(2)}, u32[]{:S(2)}) collective-permute-start(bf16[64,2048]{1,0:T(8,128)(2,1)S(1)} %get-tuple-element.26), channel_id=1, source_target_pairs={{0,2},{1,3},{2,4},{3,5},{4,6},{5,7},{6,0},{7,1},{8,10},{9,11},{10,... | collective-permute-start | bytes 786440 | tf_op jit(solution)/shard_map/ppermute | solution.py:23
  95.8 14.8 %collective-permute-start.17 = (bf16[64,2048]{1,0:T(8,128)(2,1)S(1)}, bf16[64,2048]{1,0:T(8,128)(2,1)S(1)}, u32[]{:S(2)}, u32[]{:S(2)}) collective-permute-start(bf16[64,2048]{1,0:T(8,128)(2,1)S(1)} %get-tuple-element.27), channel_id=1, source_target_pairs={{0,6},{1,7},{2,0},{3,1},{4,2},{5,3},{6,4},{7,5},{8,14},{9,15},{10,... | collective-permute-start | bytes 786440 | tf_op jit(solution)/shard_map/ppermute | solution.py:23
  96.8 17.7 %collective-permute-start.10 = (bf16[64,2048]{1,0:T(8,128)(2,1)S(1)}, bf16[64,2048]{1,0:T(8,128)(2,1)S(1)}, u32[]{:S(2)}, u32[]{:S(2)}) collective-permute-start(bf16[64,2048]{1,0:T(8,128)(2,1)S(1)} %get-tuple-element.28), channel_id=1, source_target_pairs={{0,2},{1,3},{2,4},{3,5},{4,6},{5,7},{6,0},{7,1},{8,10},{9,11},{10,... | collective-permute-start | bytes 786440 | tf_op jit(solution)/shard_map/ppermute | solution.py:23
  98.0 20.6 %collective-permute-start.12 = (bf16[64,2048]{1,0:T(8,128)(2,1)S(1)}, bf16[64,2048]{1,0:T(8,128)(2,1)S(1)}, u32[]{:S(2)}, u32[]{:S(2)}) collective-permute-start(bf16[64,2048]{1,0:T(8,128)(2,1)S(1)} %get-tuple-element.29), channel_id=1, source_target_pairs={{0,6},{1,7},{2,0},{3,1},{4,2},{5,3},{6,4},{7,5},{8,14},{9,15},{10,... | collective-permute-start | bytes 786440 | tf_op jit(solution)/shard_map/ppermute | solution.py:23
  100.3 21.4 %collective-permute-start.49 = (bf16[256,1024]{1,0:T(8,128)(2,1)}, bf16[256,1024]{1,0:T(8,128)(2,1)S(1)}, u32[]{:S(2)}, u32[]{:S(2)}) collective-permute-start(bf16[256,1024]{1,0:T(8,128)(2,1)} %collective-permute-done.47), channel_id=1, source_target_pairs={{0,8},{8,0},{16,24},{24,16},{1,9},{9,1},{17,25},{25,17},{2,10},{10... | collective-permute-start | bytes 1572872 | tf_op jit(solution)/shard_map/ppermute | solution.py:92
  103.2 18.5 %collective-permute-start.37 = (bf16[256,1024]{1,0:T(8,128)(2,1)S(1)}, bf16[256,1024]{1,0:T(8,128)(2,1)S(1)}, u32[]{:S(2)}, u32[]{:S(2)}) collective-permute-start(bf16[256,1024]{1,0:T(8,128)(2,1)S(1)} %collective-permute-done.36), channel_id=1, source_target_pairs={{0,1},{1,0},{2,3},{3,2},{4,5},{5,4},{6,7},{7,6},{8,9},{9,8},{10,11... | collective-permute-start | bytes 1572872 | tf_op jit(solution)/shard_map/ppermute | solution.py:19
  119.6 13.9 %collective-permute-start.21 = (bf16[64,2048]{1,0:T(8,128)(2,1)S(1)}, bf16[64,2048]{1,0:T(8,128)(2,1)S(1)}, u32[]{:S(2)}, u32[]{:S(2)}) collective-permute-start(bf16[64,2048]{1,0:T(8,128)(2,1)S(1)} %get-tuple-element.15), channel_id=1, source_target_pairs={{0,6},{1,7},{2,0},{3,1},{4,2},{5,3},{6,4},{7,5},{8,14},{9,15},{10,... | collective-permute-start | bytes 786440 | tf_op jit(solution)/shard_map/ppermute | solution.py:23
  121.1 13.0 %collective-permute-start.19 = (bf16[64,2048]{1,0:T(8,128)(2,1)S(1)}, bf16[64,2048]{1,0:T(8,128)(2,1)S(1)}, u32[]{:S(2)}, u32[]{:S(2)}) collective-permute-start(bf16[64,2048]{1,0:T(8,128)(2,1)S(1)} %get-tuple-element.15), channel_id=1, source_target_pairs={{0,2},{1,3},{2,4},{3,5},{4,6},{5,7},{6,0},{7,1},{8,10},{9,11},{10,... | collective-permute-start | bytes 786440 | tf_op jit(solution)/shard_map/ppermute | solution.py:23
  121.7 14.5 %collective-permute-start.18 = (bf16[64,2048]{1,0:T(8,128)(2,1)S(1)}, bf16[64,2048]{1,0:T(8,128)(2,1)S(1)}, u32[]{:S(2)}, u32[]{:S(2)}) collective-permute-start(bf16[64,2048]{1,0:T(8,128)(2,1)S(1)} %get-tuple-element.15), channel_id=1, source_target_pairs={{0,1},{1,0},{2,3},{3,2},{4,5},{5,4},{6,7},{7,6},{8,9},{9,8},{10,11... | collective-permute-start | bytes 786440 | tf_op jit(solution)/shard_map/ppermute | solution.py:19
  133.6 5.4 %collective-permute-start.24 = (bf16[32,2048]{1,0:T(8,128)(2,1)S(1)}, bf16[32,2048]{1,0:T(8,128)(2,1)S(1)}, u32[]{:S(2)}, u32[]{:S(2)}) collective-permute-start(bf16[32,2048]{1,0:T(8,128)(2,1)S(1)} %slice.179), channel_id=1, source_target_pairs={{0,6},{1,7},{2,0},{3,1},{4,2},{5,3},{6,4},{7,5},{8,14},{9,15},{10,... | collective-permute-start | bytes 393224 | tf_op jit(solution)/shard_map/ppermute | solution.py:23
  134.1 5.0 %collective-permute-start.23 = (bf16[32,2048]{1,0:T(8,128)(2,1)S(1)}, bf16[32,2048]{1,0:T(8,128)(2,1)S(1)}, u32[]{:S(2)}, u32[]{:S(2)}) collective-permute-start(bf16[32,2048]{1,0:T(8,128)(2,1)S(1)} %slice.178), channel_id=1, source_target_pairs={{0,2},{1,3},{2,4},{3,5},{4,6},{5,7},{6,0},{7,1},{8,10},{9,11},{10,... | collective-permute-start | bytes 393224 | tf_op jit(solution)/shard_map/ppermute | solution.py:23
  143.8 47.3 %collective-permute-start.38 = (bf16[512,1024]{1,0:T(8,128)(2,1)S(1)}, bf16[512,1024]{1,0:T(8,128)(2,1)S(1)}, u32[]{:S(2)}, u32[]{:S(2)}) collective-permute-start(bf16[512,1024]{1,0:T(8,128)(2,1)S(1)} %get-tuple-element.23), channel_id=1, source_target_pairs={{0,8},{8,0},{16,24},{24,16},{1,9},{9,1},{17,25},{25,17},{2,10},{10... | collective-permute-start | bytes 3145736 | tf_op jit(solution)/shard_map/ppermute | solution.py:92
  147.9 27.6 %collective-permute-start.50 = (bf16[256,512]{1,0:T(8,128)(2,1)S(1)}, bf16[256,512]{1,0:T(8,128)(2,1)S(1)}, u32[]{:S(2)}, u32[]{:S(2)}) collective-permute-start(bf16[256,512]{1,0:T(8,128)(2,1)S(1)} %get-tuple-element.30), channel_id=1, source_target_pairs={{0,8},{8,0},{16,24},{24,16},{1,9},{9,1},{17,25},{25,17},{2,10},{10... | collective-permute-start | bytes 786440 | tf_op jit(solution)/shard_map/ppermute | solution.py:92
  148.5 32.8 %collective-permute-start.54 = (bf16[256,512]{1,0:T(8,128)(2,1)S(1)}, bf16[256,512]{1,0:T(8,128)(2,1)S(1)}, u32[]{:S(2)}, u32[]{:S(2)}) collective-permute-start(bf16[256,512]{1,0:T(8,128)(2,1)S(1)} %get-tuple-element.31), channel_id=1, source_target_pairs={{0,24},{8,16},{16,8},{24,0},{1,25},{9,17},{17,9},{25,1},{2,26},{10... | collective-permute-start | bytes 786440 | tf_op jit(solution)/shard_map/ppermute | solution.py:92
  151.0 31.1 %collective-permute-start.52 = (bf16[256,512]{1,0:T(8,128)(2,1)S(1)}, bf16[256,512]{1,0:T(8,128)(2,1)S(1)}, u32[]{:S(2)}, u32[]{:S(2)}) collective-permute-start(bf16[256,512]{1,0:T(8,128)(2,1)S(1)} %get-tuple-element.32), channel_id=1, source_target_pairs={{0,16},{8,24},{16,0},{24,8},{1,17},{9,25},{17,1},{25,9},{2,18},{10... | collective-permute-start | bytes 786440 | tf_op jit(solution)/shard_map/ppermute | solution.py:92
  151.5 49.4 %collective-permute-start.42 = (bf16[512,1024]{1,0:T(8,128)(2,1)S(1)}, bf16[512,1024]{1,0:T(8,128)(2,1)S(1)}, u32[]{:S(2)}, u32[]{:S(2)}) collective-permute-start(bf16[512,1024]{1,0:T(8,128)(2,1)S(1)} %get-tuple-element.22), channel_id=1, source_target_pairs={{0,16},{8,24},{16,0},{24,8},{1,17},{9,25},{17,1},{25,9},{2,18},{10... | collective-permute-start | bytes 3145736 | tf_op jit(solution)/shard_map/ppermute | solution.py:92
  175.5 7.2 %collective-permute-start.51 = (bf16[256,512]{1,0:T(8,128)(2,1)S(1)}, bf16[256,512]{1,0:T(8,128)(2,1)S(1)}, u32[]{:S(2)}, u32[]{:S(2)}) collective-permute-start(bf16[256,512]{1,0:T(8,128)(2,1)S(1)} %collective-permute-done.50), channel_id=1, source_target_pairs={{0,1},{1,0},{2,3},{3,2},{4,5},{5,4},{6,7},{7,6},{8,9},{9,8},{10,11... | collective-permute-start | bytes 786440 | tf_op jit(solution)/shard_map/ppermute | solution.py:19
  182.7 4.9 %collective-permute-start.26 = (bf16[4,64,2048]{2,1,0:T(8,128)(2,1)S(1)}, bf16[4,64,2048]{2,1,0:T(8,128)(2,1)S(1)}, u32[]{:S(2)}, u32[]{:S(2)}) collective-permute-start(bf16[4,64,2048]{2,1,0:T(8,128)(2,1)S(1)} %fusion.15), channel_id=1, source_target_pairs={{0,1},{1,0},{2,3},{3,2},{4,5},{5,4},{6,7},{7,6},{8,9},{9,8},{10,11... | collective-permute-start | bytes 3145736 | tf_op jit(solution)/shard_map/ppermute | solution.py:19
  188.1 6.8 %collective-permute-start.27 = (bf16[32,2048]{1,0:T(8,128)(2,1)S(1)}, bf16[32,2048]{1,0:T(8,128)(2,1)S(1)}, u32[]{:S(2)}, u32[]{:S(2)}) collective-permute-start(bf16[32,2048]{1,0:T(8,128)(2,1)S(1)} %get-tuple-element.38), channel_id=1, source_target_pairs={{0,2},{1,3},{2,4},{3,5},{4,6},{5,7},{6,0},{7,1},{8,10},{9,11},{10,... | collective-permute-start | bytes 393224 | tf_op jit(solution)/shard_map/ppermute | solution.py:23
  190.4 8.3 %collective-permute-start.29 = (bf16[32,2048]{1,0:T(8,128)(2,1)S(1)}, bf16[32,2048]{1,0:T(8,128)(2,1)S(1)}, u32[]{:S(2)}, u32[]{:S(2)}) collective-permute-start(bf16[32,2048]{1,0:T(8,128)(2,1)S(1)} %get-tuple-element.39), channel_id=1, source_target_pairs={{0,6},{1,7},{2,0},{3,1},{4,2},{5,3},{6,4},{7,5},{8,14},{9,15},{10,... | collective-permute-start | bytes 393224 | tf_op jit(solution)/shard_map/ppermute | solution.py:23
  192.6 54.1 %collective-permute-start.39 = (bf16[512,1024]{1,0:T(8,128)(2,1)S(1)}, bf16[512,1024]{1,0:T(8,128)(2,1)S(1)}, u32[]{:S(2)}, u32[]{:S(2)}) collective-permute-start(bf16[512,1024]{1,0:T(8,128)(2,1)S(1)} %add_convert_fusion.1), channel_id=1, source_target_pairs={{0,16},{8,24},{16,0},{24,8},{1,17},{9,25},{17,1},{25,9},{2,18},{10... | collective-permute-start | bytes 3145736 | tf_op jit(solution)/shard_map/ppermute | solution.py:92
  198.8 12.6 %collective-permute-start.28 = (bf16[64,2048]{1,0:T(8,128)(2,1)S(1)}, bf16[64,2048]{1,0:T(8,128)(2,1)S(1)}, u32[]{:S(2)}, u32[]{:S(2)}) collective-permute-start(bf16[64,2048]{1,0:T(8,128)(2,1)S(1)} %get-tuple-element.24), channel_id=1, source_target_pairs={{0,2},{1,3},{2,4},{3,5},{4,6},{5,7},{6,0},{7,1},{8,10},{9,11},{10,... | collective-permute-start | bytes 786440 | tf_op jit(solution)/shard_map/ppermute | solution.py:23
  200.5 13.0 %collective-permute-start.30 = (bf16[64,2048]{1,0:T(8,128)(2,1)S(1)}, bf16[64,2048]{1,0:T(8,128)(2,1)S(1)}, u32[]{:S(2)}, u32[]{:S(2)}) collective-permute-start(bf16[64,2048]{1,0:T(8,128)(2,1)S(1)} %get-tuple-element.25), channel_id=1, source_target_pairs={{0,6},{1,7},{2,0},{3,1},{4,2},{5,3},{6,4},{7,5},{8,14},{9,15},{10,... | collective-permute-start | bytes 786440 | tf_op jit(solution)/shard_map/ppermute | solution.py:23
  214.6 30.1 %collective-permute-start.43 = (bf16[512,1024]{1,0:T(8,128)(2,1)S(1)}, bf16[512,1024]{1,0:T(8,128)(2,1)S(1)}, u32[]{:S(2)}, u32[]{:S(2)}) collective-permute-start(bf16[512,1024]{1,0:T(8,128)(2,1)S(1)} %add_convert_fusion), channel_id=1, source_target_pairs={{0,8},{8,0},{16,24},{24,16},{1,9},{9,1},{17,25},{25,17},{2,10},{10... | collective-permute-start | bytes 3145736 | tf_op jit(solution)/shard_map/ppermute | solution.py:92
  216.2 3.7 %collective-permute-start.32 = (f32[2048]{0:T(1024)S(1)}, f32[2048]{0:T(1024)S(1)}, u32[]{:S(2)}, u32[]{:S(2)}) collective-permute-start(f32[2048]{0:T(1024)S(1)} %add.257), channel_id=1, source_target_pairs={{0,2},{1,3},{2,0},{3,1},{4,6},{5,7},{6,4},{7,5},{8,10},{9,11},{10,... | collective-permute-start | bytes 24584 | tf_op jit(solution)/shard_map/ppermute | solution.py:99
  219.9 4.5 %collective-permute-start.33 = (f32[2048]{0:T(1024)S(1)}, f32[2048]{0:T(1024)S(1)}, u32[]{:S(2)}, u32[]{:S(2)}) collective-permute-start(f32[2048]{0:T(1024)S(1)} %add.258), channel_id=1, source_target_pairs={{0,4},{1,5},{2,6},{3,7},{4,0},{5,1},{6,2},{7,3},{8,12},{9,13},{10,... | collective-permute-start | bytes 24584 | tf_op jit(solution)/shard_map/ppermute | solution.py:99
  224.4 16.0 %collective-permute-start.34 = (f32[2048]{0:T(1024)S(1)}, f32[2048]{0:T(1024)S(1)}, u32[]{:S(2)}, u32[]{:S(2)}) collective-permute-start(f32[2048]{0:T(1024)S(1)} %add.259), channel_id=1, source_target_pairs={{0,8},{8,0},{16,24},{24,16},{1,9},{9,1},{17,25},{25,17},{2,10},{10... | collective-permute-start | bytes 24584 | tf_op jit(solution)/shard_map/ppermute | solution.py:99
  (27 other events, 143.3 us)
